TPU v7x, 32 devices: a whole 2x2x4 slice. The times are simulated.
32 devices in a mesh: pc: 4 (over z), pr: 8 (over y, x, core).
Axes of the slice: x: 2, y: 2, z: 4, core: 2. Of those that a mesh axis runs over, the one named last changes fastest.
Arguments:
- panel_in: float32 [4096, 8, 256], P('pr', 'pc')
- trail_in: float32 [4096, 2048], P('pr', 'pc')
Outputs:
- output 1: float32 [4096, 8, 256], P('pr', 'pc')
- output 2: float32 [4096, 2048], P('pr', 'pc')
All inputs are finite; a program needn't handle non-finite values.
Results may differ from a plain program's by a relative error of at most 0.001.
Values sent between devices are 32-bit elements.
A program may use at most 1 GiB of HBM per device.

v0:
```python
import jax
import jax.numpy as jnp
from jax import lax
from jax.sharding import PartitionSpec as P

PREC_HIGH = lax.Precision.HIGHEST


def solve_right(l_diag, right_side):
    return lax.linalg.triangular_solve(l_diag, right_side, left_side=False, lower=True, transpose_a=True)


def apply_update(panel_tile, trail_tile, row_panel, col_view, panel_step, row_procs, col_procs):
    local_rows, panel_dev, blk_size = panel_tile.shape
    row_start = ((panel_step + 1) // row_procs) * blk_size
    col_start = (panel_step + 1) // col_procs
    rows_part = row_panel[row_start:]
    if col_start < panel_dev:
        panel_update = jnp.einsum("rc,mbc->rmb", rows_part, col_view[col_start:panel_dev], precision=PREC_HIGH, preferred_element_type=jnp.float32)
        panel_tile = lax.dynamic_update_slice(panel_tile, panel_tile[row_start:, col_start:] - panel_update, (row_start, col_start, 0))
    trail_view = col_view[panel_dev:].reshape(trail_tile.shape[1], blk_size)
    trail_update = lax.dot_general(rows_part, trail_view, (((1,), (1,)), ((), ())), precision=PREC_HIGH, preferred_element_type=jnp.float32)
    trail_tile = lax.dynamic_update_slice(trail_tile, trail_tile[row_start:] - trail_update, (row_start, 0))
    return panel_tile, trail_tile


def solution(mesh):
    row_procs = mesh.shape["pr"]
    col_procs = mesh.shape["pc"]

    def local_part(panel_tile, trail_tile):
        local_rows, panel_dev, blk_size = panel_tile.shape
        row_blocks = local_rows // blk_size
        col_blocks = row_blocks * row_procs // col_procs
        my_row = lax.axis_index("pr")
        my_col = lax.axis_index("pc")
        block_ids = (jnp.arange(row_blocks) * row_procs + my_row)[:, None, None]
        eye_block = jnp.eye(blk_size, dtype=panel_tile.dtype)
        for panel_step in range(panel_dev * col_procs):
            owner_col = panel_step % col_procs
            local_slot = panel_step // col_procs
            owner_row = panel_step % row_procs
            diag_start = (panel_step // row_procs) * blk_size
            column = panel_tile[:, local_slot, :]
            diag_local = column[diag_start:diag_start + blk_size]
            diag_blk = lax.psum(jnp.where(my_row == owner_row, diag_local, 0.0), "pr")
            diag_blk = jnp.where(my_col == owner_col, diag_blk, eye_block)
            l_diag = jnp.linalg.cholesky(diag_blk)
            solved = solve_right(l_diag, column).reshape(row_blocks, blk_size, blk_size)
            below_diag = jnp.where(block_ids > panel_step, solved, 0.0)
            l_col = jnp.where(block_ids == panel_step, l_diag, below_diag).reshape(local_rows, blk_size)
            new_col = jnp.where(my_col == owner_col, l_col, column)
            panel_tile = lax.dynamic_update_slice(panel_tile, new_col[:, None, :], (0, local_slot, 0))
            row_panel = lax.psum(jnp.where(my_col == owner_col, below_diag.reshape(local_rows, blk_size), 0.0), "pc")
            gathered = lax.all_gather(row_panel, "pr", axis=0, tiled=False)
            by_block = gathered.reshape(row_procs, row_blocks, blk_size, blk_size).transpose(1, 0, 2, 3)
            col_view = lax.dynamic_index_in_dim(by_block.reshape(col_blocks, col_procs, blk_size, blk_size), my_col, axis=1, keepdims=False)
            panel_tile, trail_tile = apply_update(panel_tile, trail_tile, row_panel, col_view, panel_step, row_procs, col_procs)
        return panel_tile, trail_tile

    spec_panel = P("pr", "pc", None)
    spec_trail = P("pr", "pc")
    return jax.shard_map(local_part, mesh=mesh, in_specs=(spec_panel, spec_trail), out_specs=(spec_panel, spec_trail), check_vma=False)
```

profile of v0, /device:TPU:0, one launch (start us, length us, event | category | flops | bytes accessed | tf_op | source)
XLA Modules:
  0.0 1702.2 jit_solution(13200481200096503797)
XLA Ops:
  9.7 58.4 %all-reduce.18.cloned.1.call-done = f32[256,256]{0,1:T(8,128)} async-done(((f32[256,256]{0,1:T(8,128)}), f32[256,256]{0,1:T(8,128)}) %all-reduce.18.cloned.1.call-update) | async-done | bytes 262160 | tf_op jit(solution)/shard_map/psum | solution.py:46
  70.2 11.7 cholesky.382
  81.9 9.8 custom-call.25
  92.2 11.7 cholesky.399
  110.6 19.7 %custom-call.26 = f32[2,128,128]{1,2,0:T(8,128)S(1)} custom-call(f32[2,128,128]{2,1,0:T(8,128)S(1)} %get-tuple-element.54), custom_call_target="InvertDiagBlocksLowerTriangular" | custom-call | tf_op jit(solution)/shard_map/triangular_solve/custom-call.0 | solution.py:10
  132.5 36.2 %all-reduce.20.cloned.1.call-done = f32[512,256]{0,1:T(8,128)} async-done(((f32[512,256]{0,1:T(8,128)}), f32[512,256]{0,1:T(8,128)}) %all-reduce.20.cloned.1.call-update) | async-done | bytes 524304 | tf_op jit(solution)/shard_map/psum | solution.py:54
  169.5 37.2 %all-gather.17.cloned.1.call-done = f32[4096,256]{0,1:T(8,128)} async-done(((f32[512,256]{0,1:T(8,128)}), f32[4096,256]{0,1:T(8,128)}) %all-gather.17.cloned.1.call-update) | async-done | bytes 4194320 | tf_op jit(solution)/shard_map/all_gather | solution.py:55
  213.3 7.3 copy.39
  223.6 53.5 %all-reduce.22.cloned.1.call-done = f32[256,256]{0,1:T(8,128)} async-done(((f32[256,256]{0,1:T(8,128)}), f32[256,256]{0,1:T(8,128)}) %all-reduce.22.cloned.1.call-update) | async-done | bytes 262160 | tf_op jit(solution)/shard_map/psum | solution.py:46
  277.4 11.7 cholesky.416
  289.8 9.8 custom-call.27
  300.1 11.7 cholesky.433
  318.1 19.7 %custom-call.28 = f32[2,128,128]{1,2,0:T(8,128)S(1)} custom-call(f32[2,128,128]{2,1,0:T(8,128)S(1)} %get-tuple-element.55), custom_call_target="InvertDiagBlocksLowerTriangular" | custom-call | tf_op jit(solution)/shard_map/triangular_solve/custom-call.0 | solution.py:10
  340.0 38.1 %all-reduce.24.cloned.1.call-done = f32[512,256]{0,1:T(8,128)} async-done(((f32[512,256]{0,1:T(8,128)}), f32[512,256]{0,1:T(8,128)}) %all-reduce.24.cloned.1.call-update) | async-done | bytes 524304 | tf_op jit(solution)/shard_map/psum | solution.py:54
  378.9 37.0 %all-gather.19.cloned.1.call-done = f32[4096,256]{0,1:T(8,128)} async-done(((f32[512,256]{0,1:T(8,128)}), f32[4096,256]{0,1:T(8,128)}) %all-gather.19.cloned.1.call-update) | async-done | bytes 4194320 | tf_op jit(solution)/shard_map/all_gather | solution.py:55
  422.5 7.3 copy.45
  433.0 53.5 %all-reduce.26.cloned.1.call-done = f32[256,256]{0,1:T(8,128)} async-done(((f32[256,256]{0,1:T(8,128)}), f32[256,256]{0,1:T(8,128)}) %all-reduce.26.cloned.1.call-update) | async-done | bytes 262160 | tf_op jit(solution)/shard_map/psum | solution.py:46
  486.7 11.7 cholesky.450
  499.1 9.8 custom-call.29
  509.4 11.7 cholesky.467
  527.7 19.7 %custom-call.30 = f32[2,128,128]{1,2,0:T(8,128)S(1)} custom-call(f32[2,128,128]{2,1,0:T(8,128)S(1)} %get-tuple-element.56), custom_call_target="InvertDiagBlocksLowerTriangular" | custom-call | tf_op jit(solution)/shard_map/triangular_solve/custom-call.0 | solution.py:10
  549.5 39.0 %all-reduce.28.cloned.1.call-done = f32[512,256]{0,1:T(8,128)} async-done(((f32[512,256]{0,1:T(8,128)}), f32[512,256]{0,1:T(8,128)}) %all-reduce.28.cloned.1.call-update) | async-done | bytes 524304 | tf_op jit(solution)/shard_map/psum | solution.py:54
  589.4 37.2 %all-gather.21.cloned.1.call-done = f32[4096,256]{0,1:T(8,128)} async-done(((f32[512,256]{0,1:T(8,128)}), f32[4096,256]{0,1:T(8,128)}) %all-gather.21.cloned.1.call-update) | async-done | bytes 4194320 | tf_op jit(solution)/shard_map/all_gather | solution.py:55
  633.1 7.3 copy.51
  643.5 53.5 %all-reduce.30.cloned.1.call-done = f32[256,256]{0,1:T(8,128)} async-done(((f32[256,256]{0,1:T(8,128)}), f32[256,256]{0,1:T(8,128)}) %all-reduce.30.cloned.1.call-update) | async-done | bytes 262160 | tf_op jit(solution)/shard_map/psum | solution.py:46
  697.3 11.7 cholesky.484
  709.7 9.8 custom-call.31
  720.0 11.7 cholesky.501
  738.2 19.7 %custom-call.32 = f32[2,128,128]{1,2,0:T(8,128)S(1)} custom-call(f32[2,128,128]{2,1,0:T(8,128)S(1)} %get-tuple-element.57), custom_call_target="InvertDiagBlocksLowerTriangular" | custom-call | tf_op jit(solution)/shard_map/triangular_solve/custom-call.0 | solution.py:10
  760.0 40.0 %all-reduce.32.cloned.1.call-done = f32[512,256]{0,1:T(8,128)} async-done(((f32[512,256]{0,1:T(8,128)}), f32[512,256]{0,1:T(8,128)}) %all-reduce.32.cloned.1.call-update) | async-done | bytes 524304 | tf_op jit(solution)/shard_map/psum | solution.py:54
  800.7 37.1 %all-gather.23.cloned.1.call-done = f32[4096,256]{0,1:T(8,128)} async-done(((f32[512,256]{0,1:T(8,128)}), f32[4096,256]{0,1:T(8,128)}) %all-gather.23.cloned.1.call-update) | async-done | bytes 4194320 | tf_op jit(solution)/shard_map/all_gather | solution.py:55
  844.4 7.3 copy.57
  854.2 53.6 %all-reduce.34.cloned.1.call-done = f32[256,256]{0,1:T(8,128)} async-done(((f32[256,256]{0,1:T(8,128)}), f32[256,256]{0,1:T(8,128)}) %all-reduce.34.cloned.1.call-update) | async-done | bytes 262160 | tf_op jit(solution)/shard_map/psum | solution.py:46
  910.0 11.7 cholesky.518
  922.4 9.8 custom-call.33
  932.7 11.7 cholesky.535
  950.6 19.7 %custom-call.34 = f32[2,128,128]{1,2,0:T(8,128)S(1)} custom-call(f32[2,128,128]{2,1,0:T(8,128)S(1)} %get-tuple-element.58), custom_call_target="InvertDiagBlocksLowerTriangular" | custom-call | tf_op jit(solution)/shard_map/triangular_solve/custom-call.0 | solution.py:10
  972.5 36.2 %all-reduce.36.cloned.1.call-done = f32[512,256]{0,1:T(8,128)} async-done(((f32[512,256]{0,1:T(8,128)}), f32[512,256]{0,1:T(8,128)}) %all-reduce.36.cloned.1.call-update) | async-done | bytes 524304 | tf_op jit(solution)/shard_map/psum | solution.py:54
  1009.4 37.1 %all-gather.25.cloned.1.call-done = f32[4096,256]{0,1:T(8,128)} async-done(((f32[512,256]{0,1:T(8,128)}), f32[4096,256]{0,1:T(8,128)}) %all-gather.25.cloned.1.call-update) | async-done | bytes 4194320 | tf_op jit(solution)/shard_map/all_gather | solution.py:55
  1053.1 7.3 copy.61
  1062.9 53.6 %all-reduce.38.cloned.1.call-done = f32[256,256]{0,1:T(8,128)} async-done(((f32[256,256]{0,1:T(8,128)}), f32[256,256]{0,1:T(8,128)}) %all-reduce.38.cloned.1.call-update) | async-done | bytes 262160 | tf_op jit(solution)/shard_map/psum | solution.py:46
  1116.7 11.7 cholesky.552
  1129.1 9.8 custom-call.35
  1139.5 11.7 cholesky.569
  1157.6 19.7 %custom-call.36 = f32[2,128,128]{1,2,0:T(8,128)S(1)} custom-call(f32[2,128,128]{2,1,0:T(8,128)S(1)} %get-tuple-element.59), custom_call_target="InvertDiagBlocksLowerTriangular" | custom-call | tf_op jit(solution)/shard_map/triangular_solve/custom-call.0 | solution.py:10
  1179.5 38.2 %all-reduce.40.cloned.1.call-done = f32[512,256]{0,1:T(8,128)} async-done(((f32[512,256]{0,1:T(8,128)}), f32[512,256]{0,1:T(8,128)}) %all-reduce.40.cloned.1.call-update) | async-done | bytes 524304 | tf_op jit(solution)/shard_map/psum | solution.py:54
  1218.4 37.1 %all-gather.27.cloned.1.call-done = f32[4096,256]{0,1:T(8,128)} async-done(((f32[512,256]{0,1:T(8,128)}), f32[4096,256]{0,1:T(8,128)}) %all-gather.27.cloned.1.call-update) | async-done | bytes 4194320 | tf_op jit(solution)/shard_map/all_gather | solution.py:55
  1262.1 7.3 copy.65
  1271.9 53.6 %all-reduce.42.cloned.1.call-done = f32[256,256]{0,1:T(8,128)} async-done(((f32[256,256]{0,1:T(8,128)}), f32[256,256]{0,1:T(8,128)}) %all-reduce.42.cloned.1.call-update) | async-done | bytes 262160 | tf_op jit(solution)/shard_map/psum | solution.py:46
  1325.8 11.7 cholesky.586
  1338.2 9.8 custom-call.37
  1348.5 11.7 cholesky.603
  1366.4 19.7 %custom-call.38 = f32[2,128,128]{1,2,0:T(8,128)S(1)} custom-call(f32[2,128,128]{2,1,0:T(8,128)S(1)} %get-tuple-element.60), custom_call_target="InvertDiagBlocksLowerTriangular" | custom-call | tf_op jit(solution)/shard_map/triangular_solve/custom-call.0 | solution.py:10
  1388.3 39.0 %all-reduce.44.cloned.1.call-done = f32[512,256]{0,1:T(8,128)} async-done(((f32[512,256]{0,1:T(8,128)}), f32[512,256]{0,1:T(8,128)}) %all-reduce.44.cloned.1.call-update) | async-done | bytes 524304 | tf_op jit(solution)/shard_map/psum | solution.py:54
  1428.0 37.3 %all-gather.29.cloned.1.call-done = f32[4096,256]{0,1:T(8,128)} async-done(((f32[512,256]{0,1:T(8,128)}), f32[4096,256]{0,1:T(8,128)}) %all-gather.29.cloned.1.call-update) | async-done | bytes 4194320 | tf_op jit(solution)/shard_map/all_gather | solution.py:55
  1471.9 7.3 copy.69
  1481.7 53.6 %all-reduce.46.cloned.1.call-done = f32[256,256]{0,1:T(8,128)} async-done(((f32[256,256]{0,1:T(8,128)}), f32[256,256]{0,1:T(8,128)}) %all-reduce.46.cloned.1.call-update) | async-done | bytes 262160 | tf_op jit(solution)/shard_map/psum | solution.py:46
  1535.5 11.7 cholesky.620
  1547.9 9.8 custom-call.39
  1558.3 11.7 cholesky.637
  1576.5 19.7 %custom-call.40 = f32[2,128,128]{1,2,0:T(8,128)S(1)} custom-call(f32[2,128,128]{2,1,0:T(8,128)S(1)} %get-tuple-element.61), custom_call_target="InvertDiagBlocksLowerTriangular" | custom-call | tf_op jit(solution)/shard_map/triangular_solve/custom-call.0 | solution.py:10
  1600.2 39.7 %all-reduce.48.cloned.1.call-done = f32[512,256]{0,1:T(8,128)} async-done(((f32[512,256]{0,1:T(8,128)}), f32[512,256]{0,1:T(8,128)}) %all-reduce.48.cloned.1.call-update) | async-done | bytes 524304 | tf_op jit(solution)/shard_map/psum | solution.py:54
  1665.1 12.7 all-gather.31.cloned.1.call-done
  1684.4 7.3 copy.73
  (395 shorter events, 212.9 us)
Async XLA Ops:
  7.2 60.9 %all-reduce.18.cloned.1.call-start = ((), (), s32[]{:S(2)}) async-start(), calls=%async_computation | async-start | bytes 524288 | tf_op jit(solution)/shard_map/psum | solution.py:46
  9.4 159.2 %all-reduce.20.cloned.1.call-start = ((), (), s32[]{:S(2)}) async-start(), calls=%async_computation.1 | async-start | bytes 1048576 | tf_op jit(solution)/shard_map/psum | solution.py:54
  132.4 74.3 %all-gather.17.cloned.1.call-start = ((), (), s32[]{:S(2)}) async-start(), calls=%async_computation.16 | async-start | bytes 4718592 | tf_op jit(solution)/shard_map/all_gather | solution.py:55
  168.7 108.5 %all-reduce.22.cloned.1.call-start = ((), (), s32[]{:S(2)}) async-start(), calls=%async_computation.2 | async-start | bytes 524288 | tf_op jit(solution)/shard_map/psum | solution.py:46
  213.3 7.3 copy-start.1
  223.4 154.7 %all-reduce.24.cloned.1.call-start = ((), (), s32[]{:S(2)}) async-start(), calls=%async_computation.3 | async-start | bytes 1048576 | tf_op jit(solution)/shard_map/psum | solution.py:54
  339.9 76.0 %all-gather.19.cloned.1.call-start = ((), (), s32[]{:S(2)}) async-start(), calls=%async_computation.17 | async-start | bytes 4718592 | tf_op jit(solution)/shard_map/all_gather | solution.py:55
  378.1 108.4 %all-reduce.26.cloned.1.call-start = ((), (), s32[]{:S(2)}) async-start(), calls=%async_computation.4 | async-start | bytes 524288 | tf_op jit(solution)/shard_map/psum | solution.py:46
  422.5 7.3 copy-start.3
  432.7 155.9 %all-reduce.28.cloned.1.call-start = ((), (), s32[]{:S(2)}) async-start(), calls=%async_computation.5 | async-start | bytes 1048576 | tf_op jit(solution)/shard_map/psum | solution.py:54
  549.5 77.1 %all-gather.21.cloned.1.call-start = ((), (), s32[]{:S(2)}) async-start(), calls=%async_computation.18 | async-start | bytes 4718592 | tf_op jit(solution)/shard_map/all_gather | solution.py:55
  588.6 108.5 %all-reduce.30.cloned.1.call-start = ((), (), s32[]{:S(2)}) async-start(), calls=%async_computation.6 | async-start | bytes 524288 | tf_op jit(solution)/shard_map/psum | solution.py:46
  633.1 7.3 copy-start.5
  643.2 156.8 %all-reduce.32.cloned.1.call-start = ((), (), s32[]{:S(2)}) async-start(), calls=%async_computation.7 | async-start | bytes 1048576 | tf_op jit(solution)/shard_map/psum | solution.py:54
  760.0 77.9 %all-gather.23.cloned.1.call-start = ((), (), s32[]{:S(2)}) async-start(), calls=%async_computation.19 | async-start | bytes 4718592 | tf_op jit(solution)/shard_map/all_gather | solution.py:55
  800.0 107.8 %all-reduce.34.cloned.1.call-start = ((), (), s32[]{:S(2)}) async-start(), calls=%async_computation.8 | async-start | bytes 524288 | tf_op jit(solution)/shard_map/psum | solution.py:46
  844.4 7.3 copy-start
  854.1 154.6 %all-reduce.36.cloned.1.call-start = ((), (), s32[]{:S(2)}) async-start(), calls=%async_computation.9 | async-start | bytes 1048576 | tf_op jit(solution)/shard_map/psum | solution.py:54
  972.5 74.0 %all-gather.25.cloned.1.call-start = ((), (), s32[]{:S(2)}) async-start(), calls=%async_computation.20 | async-start | bytes 4718592 | tf_op jit(solution)/shard_map/all_gather | solution.py:55
  1008.7 107.8 %all-reduce.38.cloned.1.call-start = ((), (), s32[]{:S(2)}) async-start(), calls=%async_computation.10 | async-start | bytes 524288 | tf_op jit(solution)/shard_map/psum | solution.py:46
  1053.1 7.3 copy-start.7
  1062.7 154.9 %all-reduce.40.cloned.1.call-start = ((), (), s32[]{:S(2)}) async-start(), calls=%async_computation.11 | async-start | bytes 1048576 | tf_op jit(solution)/shard_map/psum | solution.py:54
  1179.4 76.0 %all-gather.27.cloned.1.call-start = ((), (), s32[]{:S(2)}) async-start(), calls=%async_computation.21 | async-start | bytes 4718592 | tf_op jit(solution)/shard_map/all_gather | solution.py:55
  1217.7 107.9 %all-reduce.42.cloned.1.call-start = ((), (), s32[]{:S(2)}) async-start(), calls=%async_computation.12 | async-start | bytes 524288 | tf_op jit(solution)/shard_map/psum | solution.py:46
  1262.1 7.3 copy-start.9
  1271.7 155.6 %all-reduce.44.cloned.1.call-start = ((), (), s32[]{:S(2)}) async-start(), calls=%async_computation.13 | async-start | bytes 1048576 | tf_op jit(solution)/shard_map/psum | solution.py:54
  1388.3 77.0 %all-gather.29.cloned.1.call-start = ((), (), s32[]{:S(2)}) async-start(), calls=%async_computation.22 | async-start | bytes 4718592 | tf_op jit(solution)/shard_map/all_gather | solution.py:55
  1427.3 108.0 %all-reduce.46.cloned.1.call-start = ((), (), s32[]{:S(2)}) async-start(), calls=%async_computation.14 | async-start | bytes 524288 | tf_op jit(solution)/shard_map/psum | solution.py:46
  1471.9 7.3 copy-start.11
  1481.5 158.4 %all-reduce.48.cloned.1.call-start = ((), (), s32[]{:S(2)}) async-start(), calls=%async_computation.15 | async-start | bytes 1048576 | tf_op jit(solution)/shard_map/psum | solution.py:54
  1535.5 105.6 %copy-start.2 = (f32[512,256]{0,1:T(8,128)S(1)}, f32[512,256]{0,1:T(8,128)}, u32[]{:S(2)}) copy-start(f32[512,256]{0,1:T(8,128)} %all-reduce.20.cloned.1.call-done) | copy-start | bytes 1572868
  1576.5 19.7 %copy-start.16 = (f32[256,256]{1,0:T(8,128)}, f32[256,256]{1,0:T(8,128)S(1)}, u32[]{:S(2)}) copy-start(f32[256,256]{1,0:T(8,128)S(1)} %get-tuple-element.661) | copy-start | bytes 786436
  1596.6 48.7 %copy-start.4 = (f32[512,256]{0,1:T(8,128)S(1)}, f32[512,256]{0,1:T(8,128)}, u32[]{:S(2)}) copy-start(f32[512,256]{0,1:T(8,128)} %all-reduce.24.cloned.1.call-done) | copy-start | bytes 1572868
  1598.4 0.7 copy-start.14
  1600.0 77.8 %all-gather.31.cloned.1.call-start = ((), (), s32[]{:S(2)}) async-start(), calls=%async_computation.23 | async-start | bytes 4718592 | tf_op jit(solution)/shard_map/all_gather | solution.py:55
  1641.1 7.2 copy-start.6
  1648.3 5.9 copy-start.8
  1651.3 5.9 copy-start.10
  1654.3 5.9 copy-start.12
  1657.2 6.4 copy-start.15
  1684.4 8.4 copy-start.17
  1693.9 1.0 copy-start.13
Sparse Core Ops, SparseCore 0:
  11.6 56.3 all-reduce.17
  132.5 36.1 all-reduce.19
  170.6 36.0 all-gather.16
  223.5 53.6 all-reduce.21
  340.0 37.9 all-reduce.23
  379.8 36.0 all-gather.18
  432.8 53.6 all-reduce.25
  549.6 38.9 all-reduce.27
  590.5 36.0 all-gather.20
  643.4 53.6 all-reduce.29
  760.1 39.8 all-reduce.31
  801.8 36.0 all-gather.22
  854.2 53.6 all-reduce.33
  972.6 36.0 all-reduce.35
  1010.4 36.0 all-gather.24
  1062.8 53.6 all-reduce.37
  1179.6 38.0 all-reduce.39
  1219.4 36.0 all-gather.26
  1271.9 53.6 all-reduce.41
  1388.4 38.8 all-reduce.43
  1429.2 36.0 all-gather.28
  1481.6 53.6 all-reduce.45
  1600.1 39.7 all-reduce.47
  1641.7 36.0 all-gather.30
where the time goes:
time: 1710 us; the launch traced here: 1700 us
  waiting for transfers between devices  1010 us (59%)
  other arithmetic  453 us (26%)
  local copies, waits for them, and re-layouts  162 us (9%)
  matrix products  42.7 us (2%)
  between operations  26.8 us (2%)
    psum x8, waiting for transfers between devices, local_part(): diag_blk = lax.psum(jnp.where(my_row == owner_row, diag_local, 0.0), 'pr')  433 us
    psum x8, waiting for transfers between devices, local_part(): lax.psum(jnp.where(my_col == owner_col, below_diag.reshape(local_rows, bl...  306 us
    another operation x55, other arithmetic, local_part(): l_diag = jnp.linalg.cholesky(diag_blk)  276 us
    all_gather x8, waiting for transfers between devices, local_part(): gathered = lax.all_gather(row_panel, 'pr', axis=0, tiled=False)  273 us
    another operation x17, other arithmetic, solve_right(): lax.linalg.triangular_solve(l_diag, right_side, left_side=False, lower=Tr...  158 us
    reshape x16, local copies, waits for them, and re-layouts, local_part(): gathered.reshape(row_procs, row_blocks, blk_size, blk_size)  111 us
  transfers between devices with their start and end apart: 24, of which 24 were waited for; matrix products, arithmetic and copies ran while one was open for 2% of the time, Pallas kernels for 0%

commit v1 on v0

v1 whole, which is shorter than its diff:
```python
import functools

import jax
import jax.numpy as jnp
from jax import lax
from jax.experimental import pallas as pl
from jax.experimental.pallas import tpu as pltpu
from jax.sharding import PartitionSpec as P

HI = lax.Precision.HIGHEST
NB = 256
B = 32
T = B // 8


def bc(v, s):
    return jnp.broadcast_to(v[s:s+1, :], (8, 128))

def factor(z, lout, wout):
    sub = lax.broadcasted_iota(jnp.int32, (8,128), 0)
    lane = lax.broadcasted_iota(jnp.int32, (8,128), 1)
    for b in range(NB//B):
        r0 = b*B; v0 = r0//128; d0 = r0-128*v0
        xa = [[z[r0+8*t:r0+8*t+8, 128*v:128*v+128] for v in range(v0,2)] for t in range(T)]
        cols = [[None]*T for _ in range(B)]
        for j in range(B):
            for t in range(j//8, T):
                cols[j][t] = jnp.broadcast_to(xa[t][0][:, d0+j:d0+j+1], (8,128))
        xs = []
        for t in range(T):
            row = list(xa[t])
            for v in range(v0):
                row.append(z[r0+8*t:r0+8*t+8, 128*v:128*v+128])
            e = jnp.where(lane < d0, xa[t][0], jnp.where(lane - d0 == sub + 8*t, 1.0, 0.0))
            row.append(e)
            xs.append(row)
        nv = len(xs[0])
        sv = [jnp.zeros((8,128), jnp.float32) for _ in range(T)]
        piv = bc(cols[0][0], 0)
        for p in range(B):
            tp, sp = divmod(p, 8)
            s = lax.rsqrt(piv)
            m = None
            if p < B-1:
                t1, s1 = divmod(p+1, 8)
                m = bc(cols[p][t1], s1)*s
                piv = bc(cols[p+1][t1], s1) - m*m
            l = [None]*T
            for t in range(tp, T):
                l[t] = cols[p][t]*s
            for j in range(p+1, B):
                mj = m if j == p+1 else bc(l[j//8], j%8)
                for t in range(j//8, T):
                    cols[j][t] = cols[j][t] - l[t]*mj
            lm = jnp.where(sub > sp, l[tp], 0.0)
            sv[tp] = jnp.where(sub == sp, s, sv[tp])
            for v in range(nv):
                u = bc(xs[tp][v], sp)*s
                if sp < 7:
                    xs[tp][v] = xs[tp][v] - lm*u
                for t in range(tp+1, T):
                    xs[t][v] = xs[t][v] - l[t]*u
        for t in range(T):
            for v in range(nv):
                xs[t][v] = xs[t][v]*sv[t]
        na = 2 - v0
        urow, rrow, wrow = [], [], []
        for t in range(T):
            a = list(xs[t][:na]); e = list(xs[t][na:])
            a0 = jnp.where(lane - d0 >= sub + 8*t, a[0], 0.0)
            ua = [jnp.zeros((8,128), jnp.float32)]*v0 + [a0] + a[1:]
            e[v0] = jnp.where(lane < d0 + B, e[v0], 0.0)
            wr = e + [jnp.zeros((8,128), jnp.float32)]*(1-v0)
            mid = jnp.where(lane < d0 + B, e[v0], a[0])
            rr = e[:v0] + [mid] + a[1:]
            urow.append(jnp.concatenate(ua, axis=1)); wrow.append(jnp.concatenate(wr, axis=1)); rrow.append(jnp.concatenate(rr, axis=1))
        U = jnp.concatenate(urow, axis=0); W = jnp.concatenate(wrow, axis=0); R = jnp.concatenate(rrow, axis=0)
        wout[r0:r0+B, :] = W
        LT = U.T
        lout[:, r0:r0+B] = LT
        lane2 = lax.broadcasted_iota(jnp.int32, (1, NB), 1)
        inb = (lane2 >= r0) & (lane2 < r0+B)
        def upd(lo, hi):
            if lo >= hi: return
            old = z[lo:hi, :]
            old = jnp.where(inb, 0.0, old)
            z[lo:hi, :] = old - lax.dot_general(LT[lo:hi], R, (((1,),(0,)),((),())), precision=HI, preferred_element_type=jnp.float32)
        upd(r0+B, min(r0+2*B, NB))
        upd(r0+2*B, NB)

def dot_nt(a, b):
    return lax.dot_general(a, b, (((1,), (1,)), ((), ())), precision=HI, preferred_element_type=jnp.float32)


def dot_nn(a, b):
    return lax.dot_general(a, b, (((1,), (0,)), ((), ())), precision=HI, preferred_element_type=jnp.float32)


def rows_at(block, count):
    return pl.ds(pl.multiple_of(block * NB, NB), count * NB)


def over_rows(first, stop, fn):
    total = stop - first
    pairs = total // 2

    def step(i, _):
        fn(first + 2 * i, 2)
        return 0

    lax.fori_loop(0, pairs, step, 0)

    @pl.when(total % 2 == 1)
    def _():
        fn(stop - 1, 1)


def local_kernel(g0, g1, low, up, trail, panel_out, trail_out, col, tt, ss, z, lo, wo, sem_a, sem_r, sem_t, sem_s):
    my_row = lax.axis_index("pr")
    my_col = lax.axis_index("pc")
    K = 8

    def copy_a(k):
        g = g0 if k < 4 else g1
        return pltpu.make_async_copy(g.at[k % 4, pl.ds(k * NB, (K - k) * NB), :], col.at[k, pl.ds(k * NB, (K - k) * NB), :], sem_a.at[k])

    def copy_r(k):
        return pltpu.make_async_copy(low.at[k % 4, k // 4], col.at[k, pl.ds(K * NB, NB), :], sem_r.at[k])

    def copy_t(k):
        return pltpu.make_async_copy(up.at[k], tt.at[k], sem_t.at[k])

    copy_s = pltpu.make_async_copy(trail, ss, sem_s)
    for k in range(K):
        copy_a(k).start()
        copy_r(k).start()
        copy_t(k).start()
    copy_s.start()
    for k in range(K):
        copy_a(k).wait()
        copy_r(k).wait()
        copy_t(k).wait()
    copy_s.wait()

    def step(k, _):
        def left(m, _):
            rhs = col[m, rows_at(k, 1), :]

            def upd(block, count):
                sl = rows_at(block, count)
                col[k, sl, :] = col[k, sl, :] - dot_nt(col[m, sl, :], rhs)

            over_rows(k, K + 1, upd)
            tt[k] = tt[k] - dot_nn(rhs, tt[m])
            return 0

        lax.fori_loop(0, k, left, 0)

        @pl.when(k == my_row)
        def _():
            trail_out[0:NB, :] = tt[k]

        z[...] = col[k, rows_at(k, 1), :]
        factor(z, lo, wo)
        col[k, rows_at(k, 1), :] = lo[...]

        def solve(block, count):
            sl = rows_at(block, count)
            col[k, sl, :] = dot_nt(col[k, sl, :], wo[...])

        over_rows(k + 1, K + 1, solve)
        tt[k] = dot_nn(wo[...], tt[k])
        ss[...] = ss[...] - dot_nn(col[k, K * NB:(K + 1) * NB, :], tt[k])

        @pl.when(my_col == k % 4)
        def _():
            slot = k // 4
            panel_out[slot, NB:, :] = col[k, K * NB:(K + 1) * NB, :]

            @pl.when(my_row >= k)
            def _():
                panel_out[slot, 0:NB, :] = col[k, rows_at(my_row, 1), :]

            @pl.when(my_row < k)
            def _():
                panel_out[slot, 0:NB, :] = jnp.zeros((NB, NB), jnp.float32)
        return 0

    lax.fori_loop(0, K, step, 0)
    trail_out[NB:, :] = ss[...]


def solution(mesh):
    vmem = pl.BlockSpec(memory_space=pltpu.VMEM)
    hbm = pl.BlockSpec(memory_space=pl.ANY)
    f32 = jnp.float32
    call = pl.pallas_call(
        local_kernel,
        out_shape=[jax.ShapeDtypeStruct((2, 512, NB), f32), jax.ShapeDtypeStruct((512, 512), f32)],
        in_specs=[hbm] * 5,
        out_specs=[vmem, vmem],
        scratch_shapes=[
            pltpu.VMEM((8, 9 * NB, NB), f32),
            pltpu.VMEM((8, NB, 512), f32),
            pltpu.VMEM((NB, 512), f32),
            pltpu.VMEM((NB, NB), f32),
            pltpu.VMEM((NB, NB), f32),
            pltpu.VMEM((NB, NB), f32),
            pltpu.SemaphoreType.DMA((8,)),
            pltpu.SemaphoreType.DMA((8,)),
            pltpu.SemaphoreType.DMA((8,)),
            pltpu.SemaphoreType.DMA,
        ],
        compiler_params=pltpu.CompilerParams(vmem_limit_bytes=60 * 1024 * 1024),
    )

    def local_part(panel_tile, trail_tile):
        slots = panel_tile.transpose(1, 0, 2)
        g0 = lax.all_gather(slots[0, :NB], ("pc", "pr"), axis=0, tiled=False).reshape(4, 8 * NB, NB)
        g1 = lax.all_gather(slots[1, :NB], ("pc", "pr"), axis=0, tiled=False).reshape(4, 8 * NB, NB)
        low = lax.all_gather(slots[:, NB:], "pc", axis=0, tiled=False)
        up = lax.all_gather(trail_tile[:NB], "pr", axis=0, tiled=False)
        p, t = call(g0, g1, low, up, trail_tile[NB:])
        return p.transpose(1, 0, 2), t

    sp, st = P("pr", "pc", None), P("pr", "pc")
    return jax.shard_map(local_part, mesh=mesh, in_specs=(sp, st), out_specs=(sp, st), check_vma=False)
```

time: 1710 us -> 402 us (0.24)
  waiting for transfers between devices: 1010 us -> 242 us
  other arithmetic: 453 us -> 0 us
  local copies, waits for them, and re-layouts: 162 us -> 8.19 us
  Pallas kernels: 0 us -> 138 us
  matrix products: 42.7 us -> 0 us
    psum x16 -> x0, waiting for transfers between devices: 740 us -> none  [the longest x8 433 us: local_part(): diag_blk = lax.psum(jnp.where(my_row == owner_row, diag_local, 0.0), 'pr')]
    another operation x72 -> x0, other arithmetic: 434 us -> none  [the longest x55 276 us: local_part(): l_diag = jnp.linalg.cholesky(diag_blk)]
    pallas_call x0 -> x1, Pallas kernels: none -> 138 us  [local_part(): p, t = call(g0, g1, low, up, trail_tile[NB:])]
    reshape x16 -> x0, local copies, waits for them, and re-layouts: 111 us -> none  [local_part(): gathered.reshape(row_procs, row_blocks, blk_size, blk_size)]
    another operation x73 -> x0, local copies, waits for them, and re-layouts: 31.8 us -> none  [the longest x57 31.6 us: solve_right(): lax.linalg.triangular_solve(l_diag, right_side, left_side=False, lower=Tr...]
    all_gather x8 -> x4, waiting for transfers between devices: 273 us -> 241 us  [the longest x1 79.7 us: local_part(): lax.all_gather(slots[1, :NB], ('pc', 'pr'), axis=0, tiled=False)]
    dot_general x15 -> x0, matrix products: 28.2 us -> none  [the longest x8 15.6 us: apply_update(): lax.dot_general(rows_part, trail_view, (((1,), (1,)), ((), ())), precisio...]
  transfers between devices with their start and end apart: 24 -> 4, of which waited for: 24 -> 4; matrix products, arithmetic and copies ran while one was open for 2% -> 1% of each run, Pallas kernels for 0% -> 0%
where the time goes in v1:
time: 402 us
  waiting for transfers between devices  242 us (60%)
  Pallas kernels  138 us (34%)
  between operations  13.8 us (3%)
  local copies, waits for them, and re-layouts  8.19 us (2%)
    pallas_call x1, Pallas kernels, local_part(): p, t = call(g0, g1, low, up, trail_tile[NB:])  138 us
    all_gather x1, waiting for transfers between devices, local_part(): lax.all_gather(slots[1, :NB], ('pc', 'pr'), axis=0, tiled=False)  79.7 us
    all_gather x1, waiting for transfers between devices, local_part(): lax.all_gather(slots[0, :NB], ('pc', 'pr'), axis=0, tiled=False)  78.5 us
    all_gather x1, waiting for transfers between devices, local_part(): low = lax.all_gather(slots[:, NB:], 'pc', axis=0, tiled=False)  45 us
    all_gather x1, waiting for transfers between devices, local_part(): up = lax.all_gather(trail_tile[:NB], 'pr', axis=0, tiled=False)  37.8 us
  transfers between devices with their start and end apart: 4, of which 4 were waited for; matrix products, arithmetic and copies ran while one was open for 1% of the time, Pallas kernels for 0%

profile of v1, /device:TPU:0, one launch (start us, length us, event | category | flops | bytes accessed | tf_op | source)
XLA Modules:
  0.0 401.7 jit_solution(16517537215128649471)
XLA Ops:
  7.2 0.0 all-gather.11.cloned.1.call-start
  7.2 1.3 copy.11
  8.5 0.8 slice.22
  9.3 0.0 all-gather.11.cloned.1.call-update
  9.4 0.0 all-gather.13.cloned.1.call-start
  9.4 2.2 fusion
  11.7 0.0 all-gather.13.cloned.1.call-update
  11.7 0.0 all-gather.9.cloned.1.call-start
  11.7 0.8 fusion.1
  12.6 0.0 all-gather.9.cloned.1.call-update
  12.6 0.0 all-gather.7.cloned.1.call-start
  12.6 0.5 all-gather.7.cloned.1.call-update
  13.2 45.0 %all-gather.11.cloned.1.call-done = f32[8,256,256]{2,1,0:T(8,128)} async-done(((f32[2,256,256]{2,1,0:T(8,128)}), f32[8,256,256]{2,1,0:T(8,128)}) %all-gather.11.cloned.1.call-update) | async-done | bytes 2097168 | tf_op jit(solution)/shard_map/all_gather | solution.py:221
  58.2 37.8 %all-gather.13.cloned.1.call-done = f32[2048,512]{1,0:T(8,128)} async-done(((f32[256,512]{1,0:T(8,128)}), f32[2048,512]{1,0:T(8,128)}) %all-gather.13.cloned.1.call-update) | async-done | bytes 4194320 | tf_op jit(solution)/shard_map/all_gather | solution.py:222
  96.0 79.7 %all-gather.9.cloned.1.call-done = f32[32,256,256]{2,1,0:T(8,128)} async-done(((f32[1,256,256]{2,1,0:T(8,128)}), f32[32,256,256]{2,1,0:T(8,128)}) %all-gather.9.cloned.1.call-update) | async-done | bytes 8388624 | tf_op jit(solution)/shard_map/all_gather | solution.py:220
  175.7 78.5 %all-gather.7.cloned.1.call-done = f32[32,256,256]{2,1,0:T(8,128)} async-done(((f32[1,256,256]{2,1,0:T(8,128)}), f32[32,256,256]{2,1,0:T(8,128)}) %all-gather.7.cloned.1.call-update) | async-done | bytes 8388624 | tf_op jit(solution)/shard_map/all_gather | solution.py:219
  254.2 138.0 %shard_map.41 = (f32[2,512,256]{2,1,0:T(8,128)}, f32[512,512]{1,0:T(8,128)}) custom-call(f32[4,2048,256]{2,1,0:T(8,128)} %bitcast.9, f32[4,2048,256]{2,1,0:T(8,128)} %bitcast.8, f32[4,2,256,256]{3,2,1,0:T(8,128)} %bitcast.13, f32[8,256,512]{2,1,0:T(8,128)} %bitcast.12, f32[256,512]{1,0:T(8,128)} %get-tuple-element.10.trail), custom_call_target="tpu_custom_call" | custom-call | tf_op jit(solution)/shard_map/pallas_call | solution.py:223
  392.2 3.0 copy.9
Async XLA Ops:
  7.2 51.0 %all-gather.11.cloned.1.call-start = ((), (), s32[]{:S(2)}) async-start(), calls=%async_computation.2 | async-start | bytes 2621440 | tf_op jit(solution)/shard_map/all_gather | solution.py:221
  9.4 86.6 %all-gather.13.cloned.1.call-start = ((), (), s32[]{:S(2)}) async-start(), calls=%async_computation.3 | async-start | bytes 4718592 | tf_op jit(solution)/shard_map/all_gather | solution.py:222
  11.7 164.0 %all-gather.9.cloned.1.call-start = ((), (), s32[]{:S(2)}) async-start(), calls=%async_computation.1 | async-start | bytes 8650752 | tf_op jit(solution)/shard_map/all_gather | solution.py:220
  12.6 241.6 %all-gather.7.cloned.1.call-start = ((), (), s32[]{:S(2)}) async-start(), calls=%async_computation | async-start | bytes 8650752 | tf_op jit(solution)/shard_map/all_gather | solution.py:219
Sparse Core Ops, SparseCore 0:
  10.1 48.0 all-gather.10
  60.6 35.3 all-gather.12
  98.9 76.7 all-gather.8
  178.4 75.7 all-gather.6

commit v2 on v1

v2 whole, which is shorter than its diff:
```python
import functools

import jax
import jax.numpy as jnp
from jax import lax
from jax.experimental import pallas as pl
from jax.experimental.pallas import tpu as pltpu
from jax.sharding import PartitionSpec as P

HI = lax.Precision.HIGHEST
NB = 256
B = 32
T = B // 8


def bc(v, s):
    return jnp.broadcast_to(v[s:s+1, :], (8, 128))

def factor(z, lout, wout, hook):
    sub = lax.broadcasted_iota(jnp.int32, (8,128), 0)
    lane = lax.broadcasted_iota(jnp.int32, (8,128), 1)
    for b in range(NB//B):
        r0 = b*B; v0 = r0//128; d0 = r0-128*v0
        hook(b)
        xa = [[z[r0+8*t:r0+8*t+8, 128*v:128*v+128] for v in range(v0,2)] for t in range(T)]
        cols = [[None]*T for _ in range(B)]
        for j in range(B):
            for t in range(j//8, T):
                cols[j][t] = jnp.broadcast_to(xa[t][0][:, d0+j:d0+j+1], (8,128))
        xs = []
        for t in range(T):
            row = list(xa[t])
            for v in range(v0):
                row.append(z[r0+8*t:r0+8*t+8, 128*v:128*v+128])
            e = jnp.where(lane < d0, xa[t][0], jnp.where(lane - d0 == sub + 8*t, 1.0, 0.0))
            row.append(e)
            xs.append(row)
        nv = len(xs[0])
        sv = [jnp.zeros((8,128), jnp.float32) for _ in range(T)]
        piv = bc(cols[0][0], 0)
        for p in range(B):
            tp, sp = divmod(p, 8)
            s = lax.rsqrt(piv)
            m = None
            if p < B-1:
                t1, s1 = divmod(p+1, 8)
                m = bc(cols[p][t1], s1)*s
                piv = bc(cols[p+1][t1], s1) - m*m
            l = [None]*T
            for t in range(tp, T):
                l[t] = cols[p][t]*s
            for j in range(p+1, B):
                mj = m if j == p+1 else bc(l[j//8], j%8)
                for t in range(j//8, T):
                    cols[j][t] = cols[j][t] - l[t]*mj
            lm = jnp.where(sub > sp, l[tp], 0.0)
            sv[tp] = jnp.where(sub == sp, s, sv[tp])
            for v in range(nv):
                u = bc(xs[tp][v], sp)*s
                if sp < 7:
                    xs[tp][v] = xs[tp][v] - lm*u
                for t in range(tp+1, T):
                    xs[t][v] = xs[t][v] - l[t]*u
        for t in range(T):
            for v in range(nv):
                xs[t][v] = xs[t][v]*sv[t]
        na = 2 - v0
        urow, rrow, wrow = [], [], []
        for t in range(T):
            a = list(xs[t][:na]); e = list(xs[t][na:])
            a0 = jnp.where(lane - d0 >= sub + 8*t, a[0], 0.0)
            ua = [jnp.zeros((8,128), jnp.float32)]*v0 + [a0] + a[1:]
            e[v0] = jnp.where(lane < d0 + B, e[v0], 0.0)
            wr = e + [jnp.zeros((8,128), jnp.float32)]*(1-v0)
            mid = jnp.where(lane < d0 + B, e[v0], a[0])
            rr = e[:v0] + [mid] + a[1:]
            urow.append(jnp.concatenate(ua, axis=1)); wrow.append(jnp.concatenate(wr, axis=1)); rrow.append(jnp.concatenate(rr, axis=1))
        U = jnp.concatenate(urow, axis=0); W = jnp.concatenate(wrow, axis=0); R = jnp.concatenate(rrow, axis=0)
        wout[r0:r0+B, :] = W
        LT = U.T
        lout[:, r0:r0+B] = LT
        lane2 = lax.broadcasted_iota(jnp.int32, (1, NB), 1)
        inb = (lane2 >= r0) & (lane2 < r0+B)
        def upd(lo, hi):
            if lo >= hi: return
            old = z[lo:hi, :]
            old = jnp.where(inb, 0.0, old)
            z[lo:hi, :] = old - lax.dot_general(LT[lo:hi], R, (((1,),(0,)),((),())), precision=HI, preferred_element_type=jnp.float32)
        upd(r0+B, min(r0+2*B, NB))
        upd(r0+2*B, NB)

MESH = pl.DeviceIdType.MESH
K = 8


def dot_nt(a, b):
    return lax.dot_general(a, b, (((1,), (1,)), ((), ())), precision=HI, preferred_element_type=jnp.float32)


def dot_nn(a, b):
    return lax.dot_general(a, b, (((1,), (0,)), ((), ())), precision=HI, preferred_element_type=jnp.float32)


def rows_at(block, count=1):
    return pl.ds(pl.multiple_of(block * NB, NB), count * NB)


def over_rows(first, stop, fn):
    total = stop - first

    def step(i, _):
        fn(first + 2 * i, 2)
        return 0

    lax.fori_loop(0, total // 2, step, 0)

    @pl.when(total % 2 == 1)
    def _():
        fn(stop - 1, 1)


def chip_kernel(panel, trail, panel_out, trail_out, col, wb, rw, tt, ss, rst, z, lo,
                rec_a, rec_w, rec_t, rec_r, rec_s, rec_o, snd_z, snd_p, snd_l, snd_w, snd_t, snd_r, snd_s, snd_o):
    c = lax.axis_index("pc")
    r = lax.axis_index("pr")
    core = r % 2
    p = r // 2
    px = 2 * (p // 2) + (1 - p % 2)
    py = 2 * (1 - p // 2) + p % 2
    pd = 3 - p
    is0 = core == 0
    is1 = core == 1

    def remote(src, dst, send, recv, c2, r2):
        return pltpu.make_async_remote_copy(src_ref=src, dst_ref=dst, send_sem=send, recv_sem=recv, device_id=(c2, r2), device_id_type=MESH)

    def z_copy(s, i):
        k = c + 4 * s
        return remote(panel.at[s, 0:NB, :], col.at[k, rows_at(r), :], snd_z.at[s, i], rec_a.at[k, r], (c + i) % 4, 2 * p)

    def z_home(s):
        k = c + 4 * s
        return pltpu.make_async_copy(panel.at[s, 0:NB, :], col.at[k, rows_at(r), :], rec_a.at[k, r])

    def z_send(s):
        k = c + 4 * s

        @pl.when((r >= k) & is0)
        def _():
            z_home(s).start()

        @pl.when((r >= k) & is1)
        def _():
            z_copy(s, 0).start()

        @pl.when(r >= k)
        def _():
            for i in (1, 3, 2):
                z_copy(s, i).start()

    def z_done(s):
        k = c + 4 * s

        @pl.when((r >= k) & is1)
        def _():
            z_copy(s, 0).wait_send()

        @pl.when(r >= k)
        def _():
            for i in (1, 2, 3):
                z_copy(s, i).wait_send()

    def t_copy(i):
        q = (p + i) % 4
        return remote(trail.at[0:NB, :], tt.at[r], snd_t.at[i], rec_t.at[r], c, 2 * q + 1)

    def r_copy(s, i):
        k = c + 4 * s
        return remote(panel.at[s, NB:2 * NB, :], rw.at[k, rows_at(core), :], snd_r.at[s, i], rec_r.at[k, core], (c + i) % 4, 2 * p + 1)

    def s_copy():
        return remote(trail.at[NB:2 * NB, :], ss.at[rows_at(core), :], snd_s, rec_s.at[core], c, r + 1)

    def other_sends():
        for i in (1, 2, 3):
            t_copy(i).start()
        for s in (0, 1):
            for i in (1, 3, 2):
                r_copy(s, i).start()

        @pl.when(is0)
        def _():
            t_copy(0).start()
            r_copy(0, 0).start()
            r_copy(1, 0).start()
            s_copy().start()

        @pl.when(is1)
        def _():
            pltpu.make_async_copy(trail.at[0:NB, :], tt.at[r], rec_t.at[r]).start()
            for s in (0, 1):
                pltpu.make_async_copy(panel.at[s, NB:2 * NB, :], rw.at[c + 4 * s, rows_at(core), :], rec_r.at[c + 4 * s, core]).start()
            pltpu.make_async_copy(trail.at[NB:2 * NB, :], ss.at[rows_at(core), :], rec_s.at[core]).start()

    def other_done():
        for i in (1, 2, 3):
            t_copy(i).wait_send()
            for s in (0, 1):
                r_copy(s, i).wait_send()

        @pl.when(is0)
        def _():
            t_copy(0).wait_send()
            r_copy(0, 0).wait_send()
            r_copy(1, 0).wait_send()
            s_copy().wait_send()

    def blk(k, j):
        return col.at[k, rows_at(j), :]

    def got_a(k, j):
        pltpu.make_async_copy(blk(k, j), blk(k, j), rec_a.at[k, j]).wait()

    def p_copy(k, j, n, q):
        return remote(blk(k, j), blk(k, j), snd_p.at[k, n], rec_a.at[k, j], c, 2 * q)

    own_sends = ((2 * p, 0, px), (2 * p, 1, py), (2 * p + 1, 2, py), (2 * p + 1, 3, px))
    fwd_sends = ((2 * px, 4, py), (2 * py + 1, 5, px))
    last_rows = (2 * px + 1, 2 * py, 2 * pd, 2 * pd + 1)

    def stage(k, lowest, sends, rows):
        for j in rows:
            @pl.when(j >= lowest)
            def _(j=j):
                got_a(k, j)
        for j, n, q in sends:
            @pl.when(j >= lowest)
            def _(j=j, n=n, q=q):
                p_copy(k, j, n, q).start()

    def stage1(k, lowest):
        stage(k, lowest, own_sends, (2 * p, 2 * p + 1))

    def stage2(k, lowest):
        stage(k, lowest, fwd_sends, (2 * px, 2 * py + 1))

    def stage3(k, lowest):
        stage(k, lowest, (), last_rows)
        for j, n, q in own_sends + fwd_sends:
            @pl.when(j >= lowest)
            def _(j=j, n=n, q=q):
                p_copy(k, j, n, q).wait_send()

    def l_copy(k, j):
        return remote(blk(k, j), blk(k, j), snd_l.at[k, j], rec_a.at[k, j], c, r + 1)

    def w_copy(k):
        return remote(wb.at[k], wb.at[k], snd_w.at[k], rec_w.at[k], c, r + 1)

    def each_row(first, fn):
        lax.fori_loop(first, K, lambda j, _: (fn(j), 0)[1], 0)

    def o_top():
        return remote(rst, trail_out.at[0:NB, :], snd_o.at[0], rec_o.at[0], c, r - 1)

    def o_low():
        return remote(ss.at[0:NB, :], trail_out.at[NB:2 * NB, :], snd_o.at[1], rec_o.at[1], c, r - 1)

    def o_row(s):
        return remote(rw.at[c + 4 * s, 0:NB, :], panel_out.at[s, NB:2 * NB, :], snd_o.at[2 + s], rec_o.at[2 + s], c, r - 1)

    z_send(0)

    @pl.when(is0)
    def _():
        @pl.when(p == 0)
        def _():
            got_a(0, 0)
            p_copy(0, 0, 0, px).start()
            p_copy(0, 0, 1, py).start()

        @pl.when(p != 0)
        def _():
            got_a(0, 0)

        @pl.when(p == 1)
        def _():
            p_copy(0, 0, 4, py).start()

        z_send(1)
        other_sends()

        def step(k, _):
            @pl.when(k > 0)
            def _():
                stage3(k, k)
                each_row(k - 1, lambda j: l_copy(k - 1, j).start())

            def left(m, _):
                rhs = col[m, rows_at(k), :]

                def upd(block, count):
                    sl = rows_at(block, count)
                    col[k, sl, :] = col[k, sl, :] - dot_nt(col[m, sl, :], rhs)

                over_rows(k, K, upd)
                return 0

            lax.fori_loop(0, k, left, 0)
            z[...] = col[k, rows_at(k), :]

            def hook(b):
                if b == 1:
                    @pl.when(k == 0)
                    def _():
                        stage1(0, 1)
                if b == 2:
                    @pl.when(k < K - 1)
                    def _():
                        stage1(k + 1, k + 1)
                if b == 5:
                    @pl.when(k == 0)
                    def _():
                        stage2(0, 1)
                if b == 7:
                    @pl.when(k < K - 1)
                    def _():
                        stage2(k + 1, k + 1)

            factor(z, lo, wb.at[k], hook)

            @pl.when(k == 0)
            def _():
                stage3(0, 1)

                @pl.when(p == 0)
                def _():
                    p_copy(0, 0, 0, px).wait_send()
                    p_copy(0, 0, 1, py).wait_send()

                @pl.when(p == 1)
                def _():
                    p_copy(0, 0, 4, py).wait_send()

            col[k, rows_at(k), :] = lo[...]
            w_copy(k).start()

            def solve(block, count):
                sl = rows_at(block, count)
                col[k, sl, :] = dot_nt(col[k, sl, :], wb[k])

            over_rows(k + 1, K, solve)
            return 0

        lax.fori_loop(0, K, step, 0)
        l_copy(K - 1, K - 1).start()

    @pl.when(is1)
    def _():
        z_send(1)
        other_sends()
        for i in (0, 1):
            pltpu.make_async_copy(ss.at[rows_at(i), :], ss.at[rows_at(i), :], rec_s.at[i]).wait()

        def step(k, _):
            pltpu.make_async_copy(tt.at[k], tt.at[k], rec_t.at[k]).wait()
            for i in (0, 1):
                pltpu.make_async_copy(rw.at[k, rows_at(i), :], rw.at[k, rows_at(i), :], rec_r.at[k, i]).wait()

            def left(m, _):
                got_a(m, k)
                lkm = col[m, rows_at(k), :]
                tt[k] = tt[k] - dot_nn(lkm, tt[m])
                rw[k] = rw[k] - dot_nt(rw[m], lkm)
                return 0

            lax.fori_loop(0, k, left, 0)

            @pl.when(k == r)
            def _():
                trail_out[0:NB, :] = tt[k]

            @pl.when(k == r - 1)
            def _():
                rst[...] = tt[k]

            pltpu.make_async_copy(wb.at[k], wb.at[k], rec_w.at[k]).wait()
            tt[k] = dot_nn(wb[k], tt[k])
            rw[k] = dot_nt(rw[k], wb[k])
            ss[...] = ss[...] - dot_nn(rw[k], tt[k])
            return 0

        lax.fori_loop(0, K, step, 0)
        o_low().start()
        o_row(0).start()
        o_row(1).start()
        o_top().start()
        trail_out[NB:2 * NB, :] = ss[NB:2 * NB, :]
        for s in (0, 1):
            panel_out[s, NB:2 * NB, :] = rw[c + 4 * s, NB:2 * NB, :]

        def diag_arrived(k, _):
            got_a(k, k)
            return 0

        lax.fori_loop(0, K, diag_arrived, 0)

    for s in (0, 1):
        k = c + 4 * s

        @pl.when(r >= k)
        def _(s=s, k=k):
            panel_out[s, 0:NB, :] = col[k, rows_at(r), :]

        @pl.when(r < k)
        def _(s=s):
            panel_out[s, 0:NB, :] = jnp.zeros((NB, NB), jnp.float32)

    z_done(0)
    z_done(1)
    other_done()

    @pl.when(is0)
    def _():
        def sent(k, _):
            w_copy(k).wait_send()
            each_row(k, lambda j: l_copy(k, j).wait_send())
            return 0

        lax.fori_loop(0, K, sent, 0)
        for ref, i in ((trail_out.at[0:NB, :], 0), (trail_out.at[NB:2 * NB, :], 1), (panel_out.at[0, NB:2 * NB, :], 2), (panel_out.at[1, NB:2 * NB, :], 3)):
            pltpu.make_async_copy(ref, ref, rec_o.at[i]).wait()

    @pl.when(is1)
    def _():
        o_low().wait_send()
        o_row(0).wait_send()
        o_row(1).wait_send()
        o_top().wait_send()


def solution(mesh):
    vmem = pl.BlockSpec(memory_space=pltpu.VMEM)
    f32 = jnp.float32
    dma = pltpu.SemaphoreType.DMA
    call = pl.pallas_call(
        chip_kernel,
        out_shape=[jax.ShapeDtypeStruct((2, 512, NB), f32), jax.ShapeDtypeStruct((512, 512), f32)],
        in_specs=[vmem, vmem],
        out_specs=[vmem, vmem],
        scratch_shapes=[
            pltpu.VMEM((K, K * NB, NB), f32),
            pltpu.VMEM((K, NB, NB), f32),
            pltpu.VMEM((K, 2 * NB, NB), f32),
            pltpu.VMEM((K, NB, 512), f32),
            pltpu.VMEM((512, 512), f32),
            pltpu.VMEM((NB, 512), f32),
            pltpu.VMEM((NB, NB), f32),
            pltpu.VMEM((NB, NB), f32),
            dma((K, K)), dma((K,)), dma((K,)), dma((K, 2)), dma((2,)), dma((4,)),
            dma((2, 4)), dma((K, 6)), dma((K, K)), dma((K,)), dma((4,)), dma((2, 4)), dma, dma((4,)),
        ],
        compiler_params=pltpu.CompilerParams(vmem_limit_bytes=60 * 1024 * 1024, has_side_effects=True),
    )

    def local_part(panel_tile, trail_tile):
        p, t = call(panel_tile.transpose(1, 0, 2), trail_tile)
        return p.transpose(1, 0, 2), t

    sp, st = P("pr", "pc", None), P("pr", "pc")
    return jax.shard_map(local_part, mesh=mesh, in_specs=(sp, st), out_specs=(sp, st), check_vma=False)
```

time: 402 us -> 199 us (0.50)
  the two profiles are of different devices: /device:TPU:0 before, /device:TPU:17 now
where the time goes in v2:
time: 199 us
  Pallas kernels  192 us (96%)
  local copies, waits for them, and re-layouts  6.34 us (3%)
    pallas_call x1, Pallas kernels, local_part(): p, t = call(panel_tile.transpose(1, 0, 2), trail_tile)  192 us
    unnamed x5, local copies, waits for them, and re-layouts  6.34 us

profile of v2, /device:TPU:17, one launch (start us, length us, event | category | flops | bytes accessed | tf_op | source)
XLA Modules:
  0.0 198.6 jit_solution(1670894902719892262)
XLA Ops:
  0.6 2.3 %copy.7 = f32[512,2,256]{2,0,1:T(8,128)} copy(f32[512,2,256]{2,1,0:T(2,128)} %param.2) | data formatting | bytes 2097152 | tf_op args[0]
  2.9 191.6 %shard_map.41 = (f32[2,512,256]{2,1,0:T(8,128)}, f32[512,512]{1,0:T(8,128)}) custom-call(f32[2,512,256]{2,1,0:T(8,128)} %bitcast.4, f32[512,512]{1,0:T(8,128)} %trail.1), custom_call_target="tpu_custom_call" | custom-call | tf_op jit(solution)/shard_map/pallas_call | solution.py:467
  194.5 0.0 copy-start
  194.5 3.1 %copy.5 = f32[512,2,256]{2,1,0:T(2,128)} copy(f32[512,2,256]{2,0,1:T(8,128)} %bitcast.5) | data formatting | bytes 2097152
  197.6 0.0 copy-done
  197.6 1.0 copy.9
Async XLA Ops:
  194.5 3.1 %copy-start = (f32[512,512]{1,0:T(8,128)S(1)}, f32[512,512]{1,0:T(8,128)}, u32[]{:S(2)}) copy-start(f32[512,512]{1,0:T(8,128)} %get-tuple-element.11) | copy-start | bytes 3145732

commit v3 on v2

--- a/solution.py
+++ b/solution.py
@@ -309,23 +309,19 @@
             lax.fori_loop(0, k, left, 0)
             z[...] = col[k, rows_at(k), :]
 
+            def at(b, when, fn):
+                if b == when[0]:
+                    @pl.when(when[1])
+                    def _():
+                        fn()
+
             def hook(b):
-                if b == 1:
-                    @pl.when(k == 0)
-                    def _():
-                        stage1(0, 1)
-                if b == 2:
-                    @pl.when(k < K - 1)
-                    def _():
-                        stage1(k + 1, k + 1)
-                if b == 5:
-                    @pl.when(k == 0)
-                    def _():
-                        stage2(0, 1)
-                if b == 7:
-                    @pl.when(k < K - 1)
-                    def _():
-                        stage2(k + 1, k + 1)
+                at(b, (0, k == 0), lambda: stage1(0, 1))
+                at(b, (1, k == 0), lambda: stage1(1, 1))
+                at(b, (3, k == 0), lambda: stage2(0, 1))
+                at(b, (5, k == 0), lambda: stage2(1, 1))
+                at(b, (2, (k > 0) & (k < K - 1)), lambda: stage2(k + 1, k + 1))
+                at(b, (6, k < K - 2), lambda: stage1(k + 2, k + 2))
 
             factor(z, lo, wb.at[k], hook)
 

time: 199 us -> 174 us (0.87)
  Pallas kernels: 192 us -> 167 us
    pallas_call x1, Pallas kernels: 192 us -> 167 us  [local_part(): p, t = call(panel_tile.transpose(1, 0, 2), trail_tile)]
where the time goes in v3:
time: 174 us
  Pallas kernels  167 us (96%)
  local copies, waits for them, and re-layouts  6.34 us (4%)
    pallas_call x1, Pallas kernels, local_part(): p, t = call(panel_tile.transpose(1, 0, 2), trail_tile)  167 us
    unnamed x5, local copies, waits for them, and re-layouts  6.34 us

profile of v3, /device:TPU:17, one launch (start us, length us, event | category | flops | bytes accessed | tf_op | source)
XLA Modules:
  0.0 174.2 jit_solution(11798942087973974983)
XLA Ops:
  0.6 2.3 %copy.7 = f32[512,2,256]{2,0,1:T(8,128)} copy(f32[512,2,256]{2,1,0:T(2,128)} %param.2) | data formatting | bytes 2097152 | tf_op args[0]
  2.9 167.2 %shard_map.41 = (f32[2,512,256]{2,1,0:T(8,128)}, f32[512,512]{1,0:T(8,128)}) custom-call(f32[2,512,256]{2,1,0:T(8,128)} %bitcast.4, f32[512,512]{1,0:T(8,128)} %trail.1), custom_call_target="tpu_custom_call" | custom-call | tf_op jit(solution)/shard_map/pallas_call | solution.py:463
  170.1 0.0 copy-start
  170.1 3.1 %copy.5 = f32[512,2,256]{2,1,0:T(2,128)} copy(f32[512,2,256]{2,0,1:T(8,128)} %bitcast.5) | data formatting | bytes 2097152
  173.2 0.0 copy-done
  173.2 1.0 copy.9
Async XLA Ops:
  170.1 3.1 %copy-start = (f32[512,512]{1,0:T(8,128)S(1)}, f32[512,512]{1,0:T(8,128)}, u32[]{:S(2)}) copy-start(f32[512,512]{1,0:T(8,128)} %get-tuple-element.11) | copy-start | bytes 3145732

commit v4 on v3

--- a/solution.py
+++ b/solution.py
@@ -119,8 +119,8 @@
         fn(stop - 1, 1)
 
 
-def chip_kernel(panel, trail, panel_out, trail_out, col, wb, rw, tt, ss, rst, z, lo,
-                rec_a, rec_w, rec_t, rec_r, rec_s, rec_o, snd_z, snd_p, snd_l, snd_w, snd_t, snd_r, snd_s, snd_o):
+def chip_kernel(panel, trail, panel_out, trail_out, ain, col, wb, rw, tt, ss, rst, z, lo,
+                rec_a, rec_w, rec_t, rec_r, rec_s, rec_o, snd_z, snd_p, snd_l, snd_w, snd_t, snd_r, snd_s, snd_o, rec_b, snd_d):
     c = lax.axis_index("pc")
     r = lax.axis_index("pr")
     core = r % 2
@@ -136,36 +136,32 @@
 
     def z_copy(s, i):
         k = c + 4 * s
-        return remote(panel.at[s, 0:NB, :], col.at[k, rows_at(r), :], snd_z.at[s, i], rec_a.at[k, r], (c + i) % 4, 2 * p)
+        return remote(panel.at[s, 0:NB, :], ain.at[k, rows_at(r), :], snd_z.at[s, i], rec_b.at[k, r], (c + i) % 4, 2 * p + 1)
 
     def z_home(s):
         k = c + 4 * s
-        return pltpu.make_async_copy(panel.at[s, 0:NB, :], col.at[k, rows_at(r), :], rec_a.at[k, r])
+        return pltpu.make_async_copy(panel.at[s, 0:NB, :], ain.at[k, rows_at(r), :], rec_b.at[k, r])
 
     def z_send(s):
-        k = c + 4 * s
-
-        @pl.when((r >= k) & is0)
-        def _():
-            z_home(s).start()
-
-        @pl.when((r >= k) & is1)
-        def _():
-            z_copy(s, 0).start()
-
-        @pl.when(r >= k)
+        @pl.when(r >= c + 4 * s)
         def _():
             for i in (1, 3, 2):
                 z_copy(s, i).start()
 
+        @pl.when((r >= c + 4 * s) & is1)
+        def _():
+            z_home(s).start()
+
+        @pl.when((r >= c + 4 * s) & is0)
+        def _():
+            z_copy(s, 0).start()
+
     def z_done(s):
-        k = c + 4 * s
-
-        @pl.when((r >= k) & is1)
+        @pl.when((r >= c + 4 * s) & is0)
         def _():
             z_copy(s, 0).wait_send()
 
-        @pl.when(r >= k)
+        @pl.when(r >= c + 4 * s)
         def _():
             for i in (1, 2, 3):
                 z_copy(s, i).wait_send()
@@ -218,38 +214,62 @@
     def blk(k, j):
         return col.at[k, rows_at(j), :]
 
+    def got_l(k, j):
+        pltpu.make_async_copy(blk(k, j), blk(k, j), rec_a.at[k, j]).wait()
+
+    def ablk(k, j):
+        return ain.at[k, rows_at(j), :]
+
     def got_a(k, j):
-        pltpu.make_async_copy(blk(k, j), blk(k, j), rec_a.at[k, j]).wait()
+        pltpu.make_async_copy(ablk(k, j), ablk(k, j), rec_b.at[k, j]).wait()
 
     def p_copy(k, j, n, q):
-        return remote(blk(k, j), blk(k, j), snd_p.at[k, n], rec_a.at[k, j], c, 2 * q)
-
-    own_sends = ((2 * p, 0, px), (2 * p, 1, py), (2 * p + 1, 2, py), (2 * p + 1, 3, px))
-    fwd_sends = ((2 * px, 4, py), (2 * py + 1, 5, px))
-    last_rows = (2 * px + 1, 2 * py, 2 * pd, 2 * pd + 1)
-
-    def stage(k, lowest, sends, rows):
-        for j in rows:
-            @pl.when(j >= lowest)
-            def _(j=j):
-                got_a(k, j)
-        for j, n, q in sends:
-            @pl.when(j >= lowest)
-            def _(j=j, n=n, q=q):
-                p_copy(k, j, n, q).start()
-
-    def stage1(k, lowest):
-        stage(k, lowest, own_sends, (2 * p, 2 * p + 1))
-
-    def stage2(k, lowest):
-        stage(k, lowest, fwd_sends, (2 * px, 2 * py + 1))
-
-    def stage3(k, lowest):
-        stage(k, lowest, (), last_rows)
-        for j, n, q in own_sends + fwd_sends:
-            @pl.when(j >= lowest)
-            def _(j=j, n=n, q=q):
-                p_copy(k, j, n, q).wait_send()
+        return remote(ablk(k, j), ablk(k, j), snd_p.at[k, n], rec_b.at[k, j], c, 2 * q + (1 if n in (0, 2) else 0))
+
+    def d_copy(k, j, n):
+        return remote(ablk(k, j), ablk(k, j), snd_d.at[k, n], rec_b.at[k, j], c, r - 1)
+
+    even, odd = 2 * p, 2 * p + 1
+    stage1_sends = ((even, (0, px), (1, py), 0), (odd, (2, py), (3, px), 1))
+    stage2_sends = ((2 * px, (4, py), None, 2), (2 * py + 1, (5, px), None, 3))
+
+    def relay(k, lowest, sends, act, first):
+        for j, one, two, n in sends:
+            @pl.when((j >= lowest) & (j >= k))
+            def _(j=j, one=one, two=two, n=n):
+                if first:
+                    got_a(k, j)
+                act(d_copy(k, j, n))
+                act(p_copy(k, j, *one))
+                if two is not None:
+                    act(p_copy(k, j, *two))
+
+    def start(copy):
+        copy.start()
+
+    def finish(copy):
+        copy.wait_send()
+
+    def stage1(k):
+        relay(k, 1, stage1_sends, start, True)
+
+    def stage2(k):
+        relay(k, 1, stage2_sends, start, True)
+
+    def first_block(act, first):
+        for here, sends in ((p == 0, stage1_sends[0]), (p == 1, stage2_sends[0])):
+            @pl.when(here)
+            def _(sends=sends):
+                j, one, two, n = sends
+                if first:
+                    got_a(0, j)
+                act(p_copy(0, j, *one))
+                if two is not None:
+                    act(p_copy(0, j, *two))
+                act(d_copy(0, j, n))
+
+    def got_rows(k, first):
+        lax.fori_loop(first, K, lambda j, _: (got_a(k, j), 0)[1], 0)
 
     def l_copy(k, j):
         return remote(blk(k, j), blk(k, j), snd_l.at[k, j], rec_a.at[k, j], c, r + 1)
@@ -270,44 +290,46 @@
         return remote(rw.at[c + 4 * s, 0:NB, :], panel_out.at[s, NB:2 * NB, :], snd_o.at[2 + s], rec_o.at[2 + s], c, r - 1)
 
     z_send(0)
+    z_send(1)
 
     @pl.when(is0)
     def _():
-        @pl.when(p == 0)
-        def _():
-            got_a(0, 0)
-            p_copy(0, 0, 0, px).start()
-            p_copy(0, 0, 1, py).start()
-
-        @pl.when(p != 0)
-        def _():
-            got_a(0, 0)
-
-        @pl.when(p == 1)
-        def _():
-            p_copy(0, 0, 4, py).start()
-
-        z_send(1)
         other_sends()
+        got_a(0, 0)
 
         def step(k, _):
+            q = jnp.maximum(k - 1, 0)
+            left = K - 1 - k
+            each = jnp.maximum(left, 1)
+
             @pl.when(k > 0)
             def _():
-                stage3(k, k)
-                each_row(k - 1, lambda j: l_copy(k - 1, j).start())
-
-            def left(m, _):
-                rhs = col[m, rows_at(k), :]
-
-                def upd(block, count):
-                    sl = rows_at(block, count)
-                    col[k, sl, :] = col[k, sl, :] - dot_nt(col[m, sl, :], rhs)
-
-                over_rows(k, K, upd)
-                return 0
-
-            lax.fori_loop(0, k, left, 0)
-            z[...] = col[k, rows_at(k), :]
+                col[q, rows_at(k), :] = dot_nt(ain[q, rows_at(k), :], wb[q])
+                w_copy(q).start()
+                l_kq = col[q, rows_at(k), :]
+                z[...] = ain[k, rows_at(k), :] - dot_nt(l_kq, l_kq)
+                l_copy(q, k).start()
+
+            @pl.when(k == 0)
+            def _():
+                z[...] = ain[0, 0:NB, :]
+
+            def solve_task(i):
+                j = jnp.where((i < left) & (k > 0), k + 1 + i, K)
+                src = jnp.where((i < left) & (k > 0), k + 1 + i, 0)
+                col[q, rows_at(j), :] = dot_nt(ain[q, rows_at(src), :], wb[q])
+
+            def update_task(t):
+                u = t - left
+                m = jnp.where(u < 0, q, u // each)
+                i = jnp.where(u < 0, t, u % each)
+                live = (left > 0) & (m < k)
+                dst_col = jnp.where(live, jnp.where(u < 0, k, k + 1), 0)
+                dst_row = jnp.where(live, k + 1 + i, K)
+                m = jnp.where(live, m, 0)
+                j = jnp.where(live, k + 1 + i, 0)
+                y = jnp.where(live, dst_col, 0)
+                ain[dst_col, rows_at(dst_row), :] = ain[dst_col, rows_at(dst_row), :] - dot_nt(col[m, rows_at(j), :], col[m, rows_at(y), :])
 
             def at(b, when, fn):
                 if b == when[0]:
@@ -316,45 +338,46 @@
                         fn()
 
             def hook(b):
-                at(b, (0, k == 0), lambda: stage1(0, 1))
-                at(b, (1, k == 0), lambda: stage1(1, 1))
-                at(b, (3, k == 0), lambda: stage2(0, 1))
-                at(b, (5, k == 0), lambda: stage2(1, 1))
-                at(b, (2, (k > 0) & (k < K - 1)), lambda: stage2(k + 1, k + 1))
-                at(b, (6, k < K - 2), lambda: stage1(k + 2, k + 2))
+                at(b, (0, k == 1), lambda: got_rows(0, 2))
+                at(b, (0, k == 1), lambda: got_rows(1, 2))
+                at(b, (2, (k > 0) & (k < K - 1)), lambda: got_rows(k + 1, k + 1))
+                if b < 2:
+                    for i in range(3):
+                        solve_task(3 * b + i)
+                else:
+                    first = (0, 3, 6, 9, 12, 14, 16)
+                    for t in range(first[b - 2], first[b - 1]):
+                        update_task(t)
 
             factor(z, lo, wb.at[k], hook)
+            col[k, rows_at(k), :] = lo[...]
 
             @pl.when(k == 0)
             def _():
-                stage3(0, 1)
-
-                @pl.when(p == 0)
-                def _():
-                    p_copy(0, 0, 0, px).wait_send()
-                    p_copy(0, 0, 1, py).wait_send()
-
-                @pl.when(p == 1)
-                def _():
-                    p_copy(0, 0, 4, py).wait_send()
-
-            col[k, rows_at(k), :] = lo[...]
-            w_copy(k).start()
-
-            def solve(block, count):
-                sl = rows_at(block, count)
-                col[k, sl, :] = dot_nt(col[k, sl, :], wb[k])
-
-            over_rows(k + 1, K, solve)
+                got_a(0, 1)
+                got_a(1, 1)
+
+            @pl.when(k > 0)
+            def _():
+                lax.fori_loop(k + 1, K, lambda j, _: (l_copy(q, j).start(), 0)[1], 0)
+
+            l_copy(k, k).start()
             return 0
 
         lax.fori_loop(0, K, step, 0)
-        l_copy(K - 1, K - 1).start()
+        w_copy(K - 1).start()
 
     @pl.when(is1)
     def _():
-        z_send(1)
         other_sends()
+        first_block(start, True)
+        stage1(0)
+        stage1(1)
+        stage2(0)
+        for n in range(2, 8):
+            stage1(n)
+            stage2(n - 1)
+        stage2(7)
         for i in (0, 1):
             pltpu.make_async_copy(ss.at[rows_at(i), :], ss.at[rows_at(i), :], rec_s.at[i]).wait()
 
@@ -364,7 +387,7 @@
                 pltpu.make_async_copy(rw.at[k, rows_at(i), :], rw.at[k, rows_at(i), :], rec_r.at[k, i]).wait()
 
             def left(m, _):
-                got_a(m, k)
+                got_l(m, k)
                 lkm = col[m, rows_at(k), :]
                 tt[k] = tt[k] - dot_nn(lkm, tt[m])
                 rw[k] = rw[k] - dot_nt(rw[m], lkm)
@@ -396,7 +419,7 @@
             panel_out[s, NB:2 * NB, :] = rw[c + 4 * s, NB:2 * NB, :]
 
         def diag_arrived(k, _):
-            got_a(k, k)
+            got_l(k, k)
             return 0
 
         lax.fori_loop(0, K, diag_arrived, 0)
@@ -429,6 +452,14 @@
 
     @pl.when(is1)
     def _():
+        first_block(finish, False)
+
+        def passed(k, _):
+            relay(k, 1, stage1_sends, finish, False)
+            relay(k, 1, stage2_sends, finish, False)
+            return 0
+
+        lax.fori_loop(0, K, passed, 0)
         o_low().wait_send()
         o_row(0).wait_send()
         o_row(1).wait_send()
@@ -445,7 +476,8 @@
         in_specs=[vmem, vmem],
         out_specs=[vmem, vmem],
         scratch_shapes=[
-            pltpu.VMEM((K, K * NB, NB), f32),
+            pltpu.VMEM((K, (K + 1) * NB, NB), f32),
+            pltpu.VMEM((K, (K + 1) * NB, NB), f32),
             pltpu.VMEM((K, NB, NB), f32),
             pltpu.VMEM((K, 2 * NB, NB), f32),
             pltpu.VMEM((K, NB, 512), f32),
@@ -454,7 +486,7 @@
             pltpu.VMEM((NB, NB), f32),
             pltpu.VMEM((NB, NB), f32),
             dma((K, K)), dma((K,)), dma((K,)), dma((K, 2)), dma((2,)), dma((4,)),
-            dma((2, 4)), dma((K, 6)), dma((K, K)), dma((K,)), dma((4,)), dma((2, 4)), dma, dma((4,)),
+            dma((2, 4)), dma((K, 6)), dma((K, K)), dma((K,)), dma((4,)), dma((2, 4)), dma, dma((4,)), dma((K, K)), dma((K, 4)),
         ],
         compiler_params=pltpu.CompilerParams(vmem_limit_bytes=60 * 1024 * 1024, has_side_effects=True),
     )

time: 174 us -> 158 us (0.908)
  the two profiles are of different devices: /device:TPU:17 before, /device:TPU:25 now
where the time goes in v4:
time: 158 us
  Pallas kernels  151 us (96%)
  local copies, waits for them, and re-layouts  6.34 us (4%)
    pallas_call x1, Pallas kernels, local_part(): p, t = call(panel_tile.transpose(1, 0, 2), trail_tile)  151 us
    unnamed x5, local copies, waits for them, and re-layouts  6.34 us

profile of v4, /device:TPU:25, one launch (start us, length us, event | category | flops | bytes accessed | tf_op | source)
XLA Modules:
  0.0 158.0 jit_solution(16265020773877371659)
XLA Ops:
  0.6 2.3 %copy.7 = f32[512,2,256]{2,0,1:T(8,128)} copy(f32[512,2,256]{2,1,0:T(2,128)} %param.2) | data formatting | bytes 2097152 | tf_op args[0]
  2.9 151.0 %shard_map.41 = (f32[2,512,256]{2,1,0:T(8,128)}, f32[512,512]{1,0:T(8,128)}) custom-call(f32[2,512,256]{2,1,0:T(8,128)} %bitcast.4, f32[512,512]{1,0:T(8,128)} %trail.1), custom_call_target="tpu_custom_call" | custom-call | tf_op jit(solution)/shard_map/pallas_call | solution.py:495
  154.0 0.0 copy-start
  154.0 3.1 %copy.5 = f32[512,2,256]{2,1,0:T(2,128)} copy(f32[512,2,256]{2,0,1:T(8,128)} %bitcast.5) | data formatting | bytes 2097152
  157.1 0.0 copy-done
  157.1 1.0 copy.9
Async XLA Ops:
  154.0 3.1 %copy-start = (f32[512,512]{1,0:T(8,128)S(1)}, f32[512,512]{1,0:T(8,128)}, u32[]{:S(2)}) copy-start(f32[512,512]{1,0:T(8,128)} %get-tuple-element.11) | copy-start | bytes 3145732
